TPU v7x, 16 devices: a whole 2x2x2 slice. The times are simulated.
16 devices in a mesh: sp: 16 (over z, y, x, core).
Axes of the slice: x: 2, y: 2, z: 2, core: 2. Of those that a mesh axis runs over, the one named last changes fastest.
Arguments:
- x: bfloat16 [32, 512, 4096], P(None, 'sp')
- dy: bfloat16 [32, 512, 4096], P(None, 'sp')
- prefix_len: int32 [32], replicated
- w_norm: bfloat16 [4096], replicated
- w_q: bfloat16 [4096, 4096], replicated
- w_k: bfloat16 [4096, 128], replicated
- w_v: bfloat16 [4096, 128], replicated
- w_o: bfloat16 [4096, 4096], replicated
Outputs:
- output 1: bfloat16 [32, 512, 4096], P(None, 'sp')
- output 2: bfloat16 [32, 512, 4096], P(None, 'sp')
- output 3: float32 [4096, 4096], replicated
- output 4: float32 [4096, 128], replicated
- output 5: float32 [4096, 128], replicated
- output 6: float32 [4096, 4096], replicated
- output 7: float32 [4096], replicated
All inputs are finite; a program needn't handle non-finite values.
Results may differ from a plain program's by a relative error of at most 0.0128496.
Values are sent between devices in bfloat16 or wider.
A program may use at most 1 GiB of HBM per device.

v0:
```python
import jax
import jax.numpy as jnp
from jax import lax
from jax.sharding import PartitionSpec as P

ROPE_THETA = 10000.0
NORM_EPS = 1e-6
MASK_FILL = -1e30


def rope_tables(positions, head_dim):
    half = head_dim // 2
    frequencies = ROPE_THETA ** (-2.0 * jnp.arange(half, dtype=jnp.float32) / head_dim)
    angles = positions.astype(jnp.float32)[:, None] * frequencies[None, :]
    return jnp.cos(angles), jnp.sin(angles)


def apply_rope(vectors, cos_tab, sin_tab):
    half = vectors.shape[-1] // 2
    first = vectors[..., :half]
    second = vectors[..., half:]
    return jnp.concatenate([first * cos_tab - second * sin_tab, second * cos_tab + first * sin_tab], axis=-1)


def rms_norm(x_f32, gain):
    inv_rms = lax.rsqrt(jnp.mean(x_f32 * x_f32, axis=-1, keepdims=True) + NORM_EPS)
    return x_f32 * inv_rms * (1.0 + gain)


def visible_mask(prefix_len, query_pos, key_pos):
    key_grid = key_pos[None, None, None, :]
    return (key_grid < prefix_len[:, None, None, None]) | (key_grid <= query_pos[None, None, :, None])


def attend_forward(q_blk, k_all, v_all, visible):
    scores = jnp.einsum('bqhe,bke->bhqk', q_blk, k_all, preferred_element_type=jnp.float32)
    attn_probs = jax.nn.softmax(jnp.where(visible, scores, MASK_FILL), axis=-1).astype(jnp.bfloat16)
    return jnp.einsum('bhqk,bke->bqhe', attn_probs, v_all, preferred_element_type=jnp.float32).astype(jnp.bfloat16)


def attend_backward(q_blk, do_blk, k_all, v_all, visible):
    scores = jnp.einsum('bqhe,bke->bhqk', q_blk, k_all, preferred_element_type=jnp.float32)
    attn_probs = jax.nn.softmax(jnp.where(visible, scores, MASK_FILL), axis=-1)
    dprobs = jnp.einsum('bqhe,bke->bhqk', do_blk, v_all, preferred_element_type=jnp.float32).astype(jnp.bfloat16).astype(jnp.float32)
    row_delta = jnp.sum(dprobs * attn_probs, axis=-1, keepdims=True)
    dscores = (attn_probs * (dprobs - row_delta)).astype(jnp.bfloat16)
    dq_blk = jnp.einsum('bhqk,bke->bqhe', dscores, k_all, preferred_element_type=jnp.float32).astype(jnp.bfloat16)
    dk_part = jnp.einsum('bhqk,bqhe->bke', dscores, q_blk, preferred_element_type=jnp.float32)
    dv_part = jnp.einsum('bhqk,bqhe->bke', attn_probs.astype(jnp.bfloat16), do_blk, preferred_element_type=jnp.float32)
    return dq_blk, dk_part, dv_part


def solution(mesh):
    groups = mesh.shape['sp']
    seq_spec = P(None, 'sp', None)
    whole = P()

    def local_block(x, dy, prefix_len, w_norm, w_q, w_k, w_v, w_o):
        batch, seq_dev, d_model = x.shape
        head_dim = w_k.shape[1]
        heads = w_q.shape[1] // head_dim
        local_heads = heads // groups
        scale = head_dim ** -0.5
        my_index = lax.axis_index('sp')
        w_q4 = w_q.reshape(d_model, groups, local_heads, head_dim)
        w_o4 = w_o.reshape(groups, local_heads, head_dim, d_model)

        x_f32 = x.astype(jnp.float32)
        normed_f32, norm_pull = jax.vjp(rms_norm, x_f32, w_norm.astype(jnp.float32))
        normed = normed_f32.astype(jnp.bfloat16)
        own_pos = my_index * seq_dev + jnp.arange(seq_dev)
        cos_tab, sin_tab = rope_tables(own_pos, head_dim)
        cos_q = cos_tab[None, None, :, None, :]
        sin_q = sin_tab[None, None, :, None, :]
        q_proj = jnp.einsum('bsd,dghe->gbshe', normed, w_q4, preferred_element_type=jnp.float32)
        q_send = (apply_rope(q_proj, cos_q, sin_q) * scale).astype(jnp.bfloat16)
        k_own = apply_rope(jnp.einsum('bsd,de->bse', normed, w_k, preferred_element_type=jnp.float32), cos_tab, sin_tab).astype(jnp.bfloat16)
        v_own = jnp.einsum('bsd,de->bse', normed, w_v, preferred_element_type=jnp.float32).astype(jnp.bfloat16)

        q_heads = lax.all_to_all(q_send, 'sp', 0, 0, tiled=True)
        k_all = lax.all_gather(k_own, 'sp', axis=1, tiled=True)
        v_all = lax.all_gather(v_own, 'sp', axis=1, tiled=True)
        key_pos = jnp.arange(seq_dev * groups)
        block_ids = jnp.arange(groups)

        def forward_block(item):
            q_blk, block_id = item
            visible = visible_mask(prefix_len, block_id * seq_dev + jnp.arange(seq_dev), key_pos)
            return attend_forward(q_blk, k_all, v_all, visible)

        o_heads = lax.map(forward_block, (q_heads, block_ids))
        o_seq = lax.all_to_all(o_heads, 'sp', 0, 0, tiled=True)
        mixed = jnp.einsum('gbshe,ghed->bsd', o_seq, w_o4, preferred_element_type=jnp.float32)
        y_out = (x_f32 + mixed).astype(jnp.bfloat16)

        d_wo = jnp.einsum('gbshe,bsd->ghed', o_seq, dy, preferred_element_type=jnp.float32).reshape(heads * head_dim, d_model)
        do_send = jnp.einsum('bsd,ghed->gbshe', dy, w_o4, preferred_element_type=jnp.float32).astype(jnp.bfloat16)
        do_heads = lax.all_to_all(do_send, 'sp', 0, 0, tiled=True)

        def backward_block(carry, item):
            dk_acc, dv_acc = carry
            q_blk, do_blk, block_id = item
            visible = visible_mask(prefix_len, block_id * seq_dev + jnp.arange(seq_dev), key_pos)
            dq_blk, dk_part, dv_part = attend_backward(q_blk, do_blk, k_all, v_all, visible)
            return (dk_acc + dk_part, dv_acc + dv_part), dq_blk

        kv_zero = jnp.zeros((batch, seq_dev * groups, head_dim), jnp.float32)
        (dk_full, dv_full), dq_heads = lax.scan(backward_block, (kv_zero, kv_zero), (q_heads, do_heads, block_ids))
        dq_seq = lax.all_to_all(dq_heads, 'sp', 0, 0, tiled=True)
        dk_own = lax.psum_scatter(dk_full, 'sp', scatter_dimension=1, tiled=True).astype(jnp.bfloat16)
        dv_own = lax.psum_scatter(dv_full, 'sp', scatter_dimension=1, tiled=True).astype(jnp.bfloat16)

        dq_proj = apply_rope(dq_seq.astype(jnp.float32) * scale, cos_q, -sin_q).astype(jnp.bfloat16)
        dk_proj = apply_rope(dk_own.astype(jnp.float32), cos_tab, -sin_tab).astype(jnp.bfloat16)
        d_wq = jnp.einsum('bsd,gbshe->dghe', normed, dq_proj, preferred_element_type=jnp.float32).reshape(d_model, heads * head_dim)
        d_wk = jnp.einsum('bsd,bse->de', normed, dk_proj, preferred_element_type=jnp.float32)
        d_wv = jnp.einsum('bsd,bse->de', normed, dv_own, preferred_element_type=jnp.float32)
        d_normed = (jnp.einsum('gbshe,dghe->bsd', dq_proj, w_q4, preferred_element_type=jnp.float32) + jnp.einsum('bse,de->bsd', dk_proj, w_k, preferred_element_type=jnp.float32) + jnp.einsum('bse,de->bsd', dv_own, w_v, preferred_element_type=jnp.float32))
        dx_norm, d_gain = norm_pull(d_normed.astype(jnp.bfloat16).astype(jnp.float32))
        dx_out = (dy.astype(jnp.float32) + dx_norm).astype(jnp.bfloat16)
        d_wq, d_wk, d_wv, d_wo, d_gain = lax.psum((d_wq, d_wk, d_wv, d_wo, d_gain), 'sp')
        return y_out, dx_out, d_wq, d_wk, d_wv, d_wo, d_gain

    return jax.shard_map(local_block, mesh=mesh, in_specs=(seq_spec, seq_spec, whole, whole, whole, whole, whole, whole), out_specs=(seq_spec, seq_spec, whole, whole, whole, whole, whole), check_vma=False)
```

profile of v0, /device:TPU:0, one launch (start us, length us, event | category | flops | bytes accessed | tf_op | source)
XLA Modules:
  0.0 2545.9 jit_solution(6436148400341234369)
XLA Ops:
  18.4 42.5 %convert_bitcast_fusion = bf16[16,32,32,2,128]{4,2,1,3,0:T(8,128)(2,1)} fusion(bf16[16,2,128,4096,1]{3,2,4,1,0:T(8,128)(2,1)} %bitcast.245, bf16[32,32,4096]{2,1,0:T(8,128)(2,1)} %param.13), kind=kOutput, calls=%fused_computation.109 | convolution fusion | flops 34363932672 | bytes 50331648 | tf_op jit(solution)/shard_map/bsd,ghed->gbshe/dot_general | solution.py:97
  67.4 5.8 fusion.104
  74.3 53.7 %reshape.367 = bf16[4096,16,2,128]{3,2,1,0:T(2,128)(2,1)} reshape(bf16[4096,4096]{1,0:T(8,128)(2,1)} %param.16) | data formatting | bytes 67108864 | tf_op jit(solution)/shard_map/reshape | solution.py:65
  128.0 43.3 %fusion.87 = f32[16,32,32,2,128]{4,2,3,0,1:T(8,128)} fusion(bf16[4096,16,2,128]{3,2,1,0:T(2,128)(2,1)} %reshape.367, bf16[32,32,4096]{2,1,0:T(8,128)(2,1)} %param.12, f32[4096]{0:T(1024)S(1)} %convert_add_fusion.1, f32[32,32]{1,0:T(8,128)S(1)} %fusion.108), kind=kOutput, calls=%fused_computation.100 | convolution fusion | flops 34376515584 | bytes 58740736 | tf_op jit(solution)/shard_map/bsd,dghe->gbshe/dot_general | solution.py:75
  171.3 17.2 multiply_subtract_fusion
  188.5 10.7 fusion.84
  199.2 9.7 copy.26
  212.8 8.9 reduce-scatter.3.cloned.1.call-start
  221.8 97.9 %all-to-all-done = bf16[16,32,32,2,128]{4,2,3,1,0:T(8,128)(2,1)} async-done(((bf16[16,32,32,2,128]{4,2,3,1,0:T(8,128)(2,1)}), bf16[16,32,32,2,128]{4,2,3,1,0:T(8,128)(2,1)}, u32[]{:S(2)}, u32[]{:S(2)}) %all-to-all-start) | async-done | bytes 8388640 | tf_op jit(solution)/shard_map/all_to_all | solution.py:80
  325.2 484.1 %while.29 = (s32[]{:T(128)}, f32[32,512,128]{2,1,0:T(8,128)}, f32[32,512,128]{2,1,0:T(8,128)}, bf16[16,32,32,2,128]{4,2,3,1,0:T(8,128)(2,1)}, s32[32]{0:T(128)S(...) while((s32[]{:T(128)}, f32[32,512,128]{2,1,0:T(8,128)}, ...), condition=%wide.region_9.10_spmd.clone.clone, body=%wide.region_5.9_spmd.clone.clone.sunk | while | flops 1368160768 | bytes 236569360 | solution.py:108
  330.9 6.1 fusion.160
  340.8 5.7 bitcast_add_fusion.6
  361.2 6.1 fusion.160
  371.1 5.7 bitcast_add_fusion.6
  391.5 6.1 fusion.160
  421.7 6.1 fusion.160
  452.0 6.1 fusion.160
  482.2 6.1 fusion.160
  512.5 6.1 fusion.160
  542.7 6.1 fusion.160
  573.0 6.1 fusion.160
  582.9 5.7 bitcast_add_fusion.6
  603.3 6.1 fusion.160
  633.5 6.1 fusion.160
  663.8 6.1 fusion.160
  694.0 6.1 fusion.160
  724.3 6.1 fusion.160
  754.5 6.1 fusion.160
  784.8 6.1 fusion.160
  819.5 216.2 %while.28 = (s32[]{:T(128)}, bf16[16,32,32,2,128]{4,2,3,1,0:T(8,128)(2,1)}, s32[32]{0:T(128)S(1)}, s32[16]{0:T(128)S(1)}, bf16[16,32,32,2,128]{4,2,3,1,0:T(8,128...) while((s32[]{:T(128)}, ...), condition=%wide.region_4.5_spmd.clone.clone, body=%wide.region_1.4_spmd.clone.clone.sunk | while | flops 543982080 | bytes 44122660 | solution.py:91
  825.2 6.1 fusion.150
  838.8 6.1 fusion.150
  852.3 6.1 fusion.150
  865.8 6.1 fusion.150
  879.3 6.1 fusion.150
  892.8 6.1 fusion.150
  906.3 6.1 fusion.150
  919.8 6.1 fusion.150
  933.3 6.1 fusion.150
  946.9 6.1 fusion.150
  960.4 6.1 fusion.150
  973.9 6.1 fusion.150
  987.4 6.1 fusion.150
  1000.9 6.1 fusion.150
  1014.4 6.1 fusion.150
  1027.9 6.1 fusion.150
  1039.5 12.0 convert_multiply_fusion.6
  1051.5 17.8 subtract_convert_fusion
  1069.4 109.8 %all-to-all-done.1 = bf16[16,32,32,2,128]{4,2,3,1,0:T(8,128)(2,1)} async-done(((bf16[16,32,32,2,128]{4,2,3,1,0:T(8,128)(2,1)}), bf16[16,32,32,2,128]{4,2,3,1,0:T(8,128)(2,1)}, u32[]{:S(2)}, u32[]{:S(2)}) %all-to-all-start.1) | async-done | bytes 8388640 | tf_op jit(solution)/shard_map/all_to_all | solution.py:92
  1179.2 45.5 %fusion.90 = f32[16,2,128,4096,1]{3,2,1,4,0:T(8,128)} fusion(bf16[16,32,32,2,128]{4,2,3,1,0:T(8,128)(2,1)} %all-to-all-done.1, bf16[32,32,4096]{2,1,0:T(8,128)(2,1)} %param.13), kind=kOutput, calls=%fused_computation.101 | convolution fusion | flops 34359738368 | bytes 83886080 | tf_op jit(solution)/shard_map/gbshe,bsd->ghed/dot_general | solution.py:96
  1225.4 48.3 %fusion.92 = f32[4096,16,2,128,1]{0,3,2,1,4:T(8,128)} fusion(bf16[16,32,32,2,64]{4,2,3,0,1:T(8,128)(2,1)} %get-tuple-element.292, bf16[16,32,32,2,64]{4,2,3,0,1:T(8,128)(2,1)} %get-tuple-element.291, bf16[32,32,4096]{2,1,0:T(8,128)(2,1)} %param.12, f32[4096]{0:T(1024)S(1)} %copy-done.23, f32[32,32]{1,0:T(8,128)S(1)} %copy-done.26), kind=kOutput, calls=%fused_computation.104 | convolution fusion | flops 34393292800 | bytes 83906560 | tf_op jit(solution)/shard_map/bsd,gbshe->dghe/dot_general | solution.py:115
  1273.7 65.8 %copy.32 = f32[4096,4096]{1,0:T(8,128)} copy(f32[4096,4096]{0,1:T(8,128)} %bitcast.22) | data formatting | bytes 134217728 | tf_op jit(solution)/shard_map/reshape | solution.py:115
  1341.6 7.7 convolution_bitcast_fusion.1
  1349.4 7.6 convolution_bitcast_fusion
  1357.0 42.2 %fusion.80 = bf16[32,32,4096]{2,1,0:T(8,128)(2,1)} fusion(bf16[32,32,4096]{2,1,0:T(8,128)(2,1)} %param.12, bf16[16,32,32,2,128]{4,2,3,1,0:T(8,128)(2,1)} %all-to-all-done.1, bf16[16,2,128,4096,1]{3,2,1,4,0:T(8,128)(2,1)} %bitcast.246), kind=kOutput, calls=%fused_computation.88 | convolution fusion | flops 34372321280 | bytes 58720256 | tf_op jit(solution)/shard_map/gbshe,ghed->bsd/dot_general | solution.py:93
  1399.2 8.1 fusion.102
  1407.4 8.5 fusion.99
  1415.9 60.3 %fusion.76 = (f32[4096]{0:T(1024)S(1)}, f32[32,32]{1,0:T(8,128)S(1)}, bf16[32,32,4096]{2,1,0:T(8,128)(2,1)}) fusion(bf16[32,32,4096]{2,1,0:T(8,128)(2,1)} %param.12, f32[32,32]{1,0:T(8,128)S(1)} %copy-done.27, f32[4096]{0:T(1024)S(1)} %copy-done.24, f32[32,32,4096]{2,1,0:T(8,128)} %fusion.99, f32[32,32,4096]{2,1,0:T(8,128)} %fusion.102, ...), kind=kOutput, calls=%fused_computation.84 | convolution fusion | flops 34422648832 | bytes 92315648 | tf_op jit(solution)/shard_map/gbshe,dghe->bsd/dot_general | solution.py:118
  1476.1 38.7 %psum.39 = f32[4096]{0:T(1024)} all-reduce(f32[4096]{0:T(1024)S(1)} %get-tuple-element.242), channel_id=1, replica_groups=mesh['sp'=16] {'sp'}, use_global_device_ids=true, to_apply=%region_18.19 | all-reduce | flops 4096 | bytes 32768 | tf_op jit(solution)/shard_map/psum | solution.py:121
  1514.9 13.7 fusion.78
  1528.6 290.0 %all-reduce.4.cloned.1.call-done = f32[4096,4096]{1,0:T(8,128)} async-done(((f32[4096,4096]{1,0:T(8,128)}), f32[4096,4096]{1,0:T(8,128)}) %all-reduce.4.cloned.1.call-update) | async-done | bytes 67108880 | tf_op jit(solution)/shard_map/psum | solution.py:121
  1818.6 627.5 %all-reduce.6.cloned.1.call-done = (f32[4096,4096]{1,0:T(8,128)}, f32[4096,128]{1,0:T(8,128)}, f32[4096,128]{1,0:T(8,128)}) async-done(((f32[4096,4096]{1,0:T(8,128)}, f32[4096,128]{1,0:T(8,128)}, f32[4096,128]{1,0:T(8,128)}), (f32[4096,4096]{1,0:T(8,128)}, f32[4096,128]{1,0:T(8,128)}, f32[4096,128]{1,0:T(8,128)})) %all-reduce.6.cloned.1.call-update) | async-done | bytes 71303184 | tf_op jit(solution)/shard_map/psum | solution.py:121
  2446.1 44.1 %copy.105 = f32[4096,4096]{1,0:T(8,128)} copy(f32[4096,4096]{1,0:T(8,128)} %get-tuple-element.495) | data formatting | bytes 134217728
  2494.6 44.1 %copy.108 = f32[4096,4096]{1,0:T(8,128)} copy(f32[4096,4096]{1,0:T(8,128)} %all-reduce.4.cloned.1.call-done) | data formatting | bytes 134217728
  (666 shorter events, 513.5 us)
Async XLA Ops:
  7.2 60.2 %copy-start = (bf16[4096,128]{1,0:T(8,128)(2,1)S(1)}, bf16[4096,128]{1,0:T(8,128)(2,1)}, u32[]{:S(2)}) copy-start(bf16[4096,128]{1,0:T(8,128)(2,1)} %param.17) | copy-start | bytes 3145732
  7.2 214.6 %all-gather.5.cloned.1.call-start = ((), (), s32[]{:S(2)}) async-start(), calls=%async_computation.7 | async-start | bytes 4456448 | tf_op jit(solution)/shard_map/all_gather | solution.py:82
  7.2 6.8 copy-start.3
  8.1 119.9 %copy-start.22 = (f32[4096]{0:T(1024)}, f32[4096]{0:T(1024)S(1)}, u32[]{:S(2)}) copy-start(f32[4096]{0:T(1024)S(1)} %convert_add_fusion.1) | copy-start | bytes 49156
  14.0 114.0 %copy-start.25 = (f32[32,32]{1,0:T(8,128)}, f32[32,32]{1,0:T(8,128)S(1)}, u32[]{:S(2)}) copy-start(f32[32,32]{1,0:T(8,128)S(1)} %fusion.108) | copy-start | bytes 12292
  60.9 148.0 %all-to-all-start.2 = ((bf16[16,32,32,2,128]{4,2,1,3,0:T(8,128)(2,1)}), bf16[16,32,32,2,128]{4,2,1,3,0:T(8,128)(2,1)}, u32[]{:S(2)}, u32[]{:S(2)}) async-start(bf16[16,32,32,2,128]{4,2,1,3,0:T(8,128)(2,1)} %convert_bitcast_fusion), calls=%async_computation.2 | async-start | bytes 16777216 | tf_op jit(solution)/shard_map/all_to_all | solution.py:98
  66.3 155.5 %all-gather.3.cloned.1.call-start = ((), (), s32[]{:S(2)}) async-start(), calls=%async_computation.6 | async-start | bytes 4456448 | tf_op jit(solution)/shard_map/all_gather | solution.py:81
  128.0 43.3 %copy-start.13 = (f32[32,64]{1,0:T(8,128)S(1)}, f32[32,64]{1,0:T(8,128)}, u32[]{:S(2)}) copy-start(f32[32,64]{1,0:T(8,128)} %copy-done.12) | copy-start | bytes 24580
  128.0 43.3 %copy-start.21 = (f32[32,64]{1,0:T(8,128)S(1)}, f32[32,64]{1,0:T(8,128)}, u32[]{:S(2)}) copy-start(f32[32,64]{1,0:T(8,128)} %copy-done.20) | copy-start | bytes 24580
  208.9 110.7 %all-to-all-start = ((bf16[16,32,32,2,128]{4,2,3,1,0:T(8,128)(2,1)}), bf16[16,32,32,2,128]{4,2,3,1,0:T(8,128)(2,1)}, u32[]{:S(2)}, u32[]{:S(2)}) async-start(bf16[16,32,32,2,128]{4,2,3,1,0:T(8,128)(2,1)} %copy.26), calls=%async_computation | async-start | bytes 16777216 | tf_op jit(solution)/shard_map/all_to_all | solution.py:80
  212.8 112.5 %copy-start.28 = (s32[32]{0:T(128)S(1)}, s32[32]{0:T(128)}, u32[]{:S(2)}) copy-start(s32[32]{0:T(128)} %param.14) | copy-start | bytes 388
  212.8 1126.7 %reduce-scatter.3.cloned.1.call-start = ((), (), s32[]{:S(2)}) async-start(), calls=%async_computation.8 | async-start | bytes 8912896 | tf_op jit(solution)/shard_map/reduce_scatter | solution.py:110
  326.9 10.2 copy-start.29
  339.9 6.6 slice-start
  357.1 10.2 copy-start.29
  370.2 6.6 slice-start
  387.4 10.2 copy-start.29
  400.5 6.6 slice-start
  417.6 10.2 copy-start.29
  447.9 10.2 copy-start.29
  478.1 10.2 copy-start.29
  508.4 10.2 copy-start.29
  538.7 10.2 copy-start.29
  568.9 10.2 copy-start.29
  599.2 10.2 copy-start.29
  629.4 10.2 copy-start.29
  659.7 10.2 copy-start.29
  689.9 10.2 copy-start.29
  720.2 10.2 copy-start.29
  750.5 10.2 copy-start.29
  780.7 10.2 copy-start.29
  809.4 226.4 %all-to-all-start.3 = ((bf16[16,32,32,2,128]{4,2,3,1,0:T(8,128)(2,1)}), bf16[16,32,32,2,128]{4,2,3,1,0:T(8,128)(2,1)}, u32[]{:S(2)}, u32[]{:S(2)}) async-start(bf16[16,32,32,2,128]{4,2,3,1,0:T(8,128)(2,1)} %get-tuple-element.115), calls=%async_computation.3 | async-start | bytes 16777216 | tf_op jit(solution)/shard_map/all_to_all | solution.py:109
  813.4 536.0 %reduce-scatter.5.cloned.1.call-start = ((), (), s32[]{:S(2)}) async-start(), calls=%async_computation.9 | async-start | bytes 8912896 | tf_op jit(solution)/shard_map/reduce_scatter | solution.py:111
  821.2 10.2 copy-start.30
  834.7 10.2 copy-start.30
  848.2 10.2 copy-start.30
  861.7 10.2 copy-start.30
  875.2 10.2 copy-start.30
  888.7 10.2 copy-start.30
  902.2 10.2 copy-start.30
  915.7 10.2 copy-start.30
  929.3 10.2 copy-start.30
  942.8 10.2 copy-start.30
  956.3 10.2 copy-start.30
  969.8 10.2 copy-start.30
  983.3 10.2 copy-start.30
  996.8 10.2 copy-start.30
  1010.3 10.2 copy-start.30
  1023.8 10.2 copy-start.30
  1035.7 143.5 %all-to-all-start.1 = ((bf16[16,32,32,2,128]{4,2,3,1,0:T(8,128)(2,1)}), bf16[16,32,32,2,128]{4,2,3,1,0:T(8,128)(2,1)}, u32[]{:S(2)}, u32[]{:S(2)}) async-start(bf16[16,32,32,2,128]{4,2,3,1,0:T(8,128)(2,1)} %get-tuple-element.114), calls=%async_computation.1 | async-start | bytes 16777216 | tf_op jit(solution)/shard_map/all_to_all | solution.py:92
  1039.5 12.1 copy-start.14
  1039.5 12.1 copy-start.16
  1039.5 779.1 %all-reduce.4.cloned.1.call-start = ((), (), s32[]{:S(2)}) async-start(), calls=%async_computation.10 | async-start | bytes 134217728 | tf_op jit(solution)/shard_map/psum | solution.py:121
  1224.7 1221.4 %all-reduce.6.cloned.1.call-start = ((), (), s32[]{:S(2)}) async-start(), calls=%async_computation.11 | async-start | bytes 142606336 | tf_op jit(solution)/shard_map/psum | solution.py:121
  1273.7 66.9 %copy-start.15 = (f32[32,64]{1,0:T(8,128)S(1)}, f32[32,64]{1,0:T(8,128)}, u32[]{:S(2)}) copy-start(f32[32,64]{1,0:T(8,128)} %copy-done.12) | copy-start | bytes 24580
  1273.7 66.9 %copy-start.17 = (f32[32,64]{1,0:T(8,128)S(1)}, f32[32,64]{1,0:T(8,128)}, u32[]{:S(2)}) copy-start(f32[32,64]{1,0:T(8,128)} %get-tuple-element.299) | copy-start | bytes 24580
  1357.0 42.2 %copy-start.7 = (bf16[32,32,64]{2,1,0:T(8,128)(2,1)S(1)}, bf16[32,32,64]{2,1,0:T(8,128)(2,1)}, u32[]{:S(2)}) copy-start(bf16[32,32,64]{2,1,0:T(8,128)(2,1)} %copy-done.6) | copy-start | bytes 393220
  1357.0 42.2 %copy-start.9 = (bf16[32,32,64]{2,1,0:T(8,128)(2,1)S(1)}, bf16[32,32,64]{2,1,0:T(8,128)(2,1)}, u32[]{:S(2)}) copy-start(bf16[32,32,64]{2,1,0:T(8,128)(2,1)} %copy-done.8) | copy-start | bytes 393220
  1399.2 8.2 copy-start.10
  1399.2 8.2 copy-start.11
  1407.3 8.5 copy-start.24
  1407.3 8.5 copy-start.27
  1415.9 99.0 %copy-start.19 = (f32[32,32]{1,0:T(8,128)S(1)}, f32[32,32]{1,0:T(8,128)}, u32[]{:S(2)}) copy-start(f32[32,32]{1,0:T(8,128)} %copy-done.18) | copy-start | bytes 12292
  2446.1 47.2 %copy-start.5 = (f32[4096,128]{1,0:T(8,128)S(1)}, f32[4096,128]{1,0:T(8,128)}, u32[]{:S(2)}) copy-start(f32[4096,128]{1,0:T(8,128)} %get-tuple-element.497) | copy-start | bytes 6291460
  (116 other events, 531.7 us)
Sparse Core Ops, SparseCore 0:
  18.5 40.0 all-gather.4
  74.4 89.8 all-gather.2
  809.5 181.6 reduce-scatter.2
  993.3 133.1 reduce-scatter.4
  1224.8 593.7 all-reduce.3
  1825.5 620.5 all-reduce.5
where the time goes:
time: 2560 us; the launch traced here: 2550 us
  waiting for transfers between devices  1130 us (44%)
  matrix products  730 us (29%)
  other arithmetic  301 us (12%)
  local copies, waits for them, and re-layouts  285 us (11%)
  blocking collectives  38.7 us (2%)
  starting transfers between devices  26.7 us (1%)
    psum x2, waiting for transfers between devices, local_block(): lax.psum((d_wq, d_wk, d_wv, d_wo, d_gain), 'sp')  918 us
    all_to_all x1, waiting for transfers between devices, local_block(): o_seq = lax.all_to_all(o_heads, 'sp', 0, 0, tiled=True)  110 us
    all_to_all x1, waiting for transfers between devices, local_block(): q_heads = lax.all_to_all(q_send, 'sp', 0, 0, tiled=True)  97.9 us
    sub x16, other arithmetic, attend_forward(): jax.nn.softmax(jnp.where(visible, scores, MASK_FILL), axis=-1)  97.3 us
    sub x16, other arithmetic, attend_backward(): attn_probs = jax.nn.softmax(jnp.where(visible, scores, MASK_FILL), axis=-1)  97.3 us
    unnamed x56, local copies, waits for them, and re-layouts  94.7 us
    dot_general x16, matrix products, attend_backward(): jnp.einsum('bhqk,bqhe->bke', attn_probs.astype(jnp.bfloat16), do_blk, pre...  90.7 us
    dot_general x16, matrix products, attend_backward(): jnp.einsum('bhqk,bqhe->bke', dscores, q_blk, preferred_element_type=jnp.f...  76.6 us
  transfers between devices with their start and end apart: 10, of which 4 were waited for; matrix products, arithmetic and copies ran while one was open for 29% of the time, Pallas kernels for 0%

commit v1 on v0

v1 whole, which is shorter than its diff:
```python
import functools
import jax
import jax.numpy as jnp
from jax import lax
from jax.experimental import pallas as pl
from jax.experimental.pallas import tpu as pltpu
from jax.sharding import PartitionSpec as P

ROPE_THETA = 10000.0
NORM_EPS = 1e-6
MASK_FILL = -1e30
GROUP_HEADS = 8


def rope_tables(positions, head_dim):
    half = head_dim // 2
    frequencies = ROPE_THETA ** (-2.0 * jnp.arange(half, dtype=jnp.float32) / head_dim)
    angles = positions.astype(jnp.float32)[:, None] * frequencies[None, :]
    return jnp.cos(angles), jnp.sin(angles)


def apply_rope(vectors, cos_tab, sin_tab):
    half = vectors.shape[-1] // 2
    first = vectors[..., :half]
    second = vectors[..., half:]
    return jnp.concatenate([first * cos_tab - second * sin_tab, second * cos_tab + first * sin_tab], axis=-1)


def rms_norm(x_f32, gain):
    inv_rms = lax.rsqrt(jnp.mean(x_f32 * x_f32, axis=-1, keepdims=True) + NORM_EPS)
    return x_f32 * inv_rms * (1.0 + gain)


def attention_kernel(heads, scale, prefix_ref, base_ref, q_ref, do_ref, kv_ref, cos_ref, sin_ref, cost_ref, sint_ref,
                     o_ref, dq_ref, dk_ref, dv_ref, cap_ref):
    b = pl.program_id(0)
    tokens = q_ref.shape[1]
    e = kv_ref.shape[2] // 2
    n_keys = kv_ref.shape[1]
    rows = GROUP_HEADS * tokens
    prefix = prefix_ref[b]
    key_pos = lax.broadcasted_iota(jnp.int32, (n_keys, rows), 0)
    token = lax.rem(lax.broadcasted_iota(jnp.int32, (n_keys, rows), 1), tokens) + base_ref[0]
    cap_ref[...] = jnp.where((key_pos < prefix) | (key_pos <= token), jnp.inf, MASK_FILL)

    k = kv_ref[0, :, :e]
    v = kv_ref[0, :, e:]
    k_t = k.T
    v_t = v.T
    cos = cos_ref[...]
    sin = sin_ref[...]
    nt = (((1,), (1,)), ((), ()))
    nn = (((1,), (0,)), ((), ()))
    f32 = jnp.float32
    dk = None
    for g in range(heads // GROUP_HEADS):
        cols = [slice((g * GROUP_HEADS + i) * e, (g * GROUP_HEADS + i + 1) * e) for i in range(GROUP_HEADS)]
        q_raw = jnp.concatenate([q_ref[0, :, c] for c in cols], axis=0)
        q = ((q_raw * cos + pltpu.roll(q_raw, e // 2, 1) * sin) * scale).astype(jnp.bfloat16)
        do = jnp.concatenate([do_ref[0, :, c] for c in cols], axis=0)
        s = jnp.minimum(lax.dot_general(k, q, nt, preferred_element_type=f32), cap_ref[...])
        p = jnp.exp(s - jnp.max(s, axis=0, keepdims=True))
        p = p * (1.0 / jnp.sum(p, axis=0, keepdims=True))
        p_b = p.astype(jnp.bfloat16)
        dp = lax.dot_general(v, do, nt, preferred_element_type=f32).astype(jnp.bfloat16).astype(f32)
        delta = jnp.sum(dp * p, axis=0, keepdims=True)
        ds = (p * (dp - delta)).astype(jnp.bfloat16)
        o_t = lax.dot_general(v_t, p_b, nn, preferred_element_type=f32)
        dq_t = lax.dot_general(k_t, ds, nn, preferred_element_type=f32).astype(jnp.bfloat16).astype(f32) * scale
        dq_t = dq_t * cost_ref[...] - jnp.concatenate([dq_t[e // 2:], dq_t[:e // 2]], axis=0) * sint_ref[...]
        o = o_t.T.astype(jnp.bfloat16)
        dq = dq_t.T.astype(jnp.bfloat16)
        for i, c in enumerate(cols):
            o_ref[0, :, c] = o[i * tokens:(i + 1) * tokens]
            dq_ref[0, :, c] = dq[i * tokens:(i + 1) * tokens]
        dk_g = lax.dot_general(ds, q, nn, preferred_element_type=f32)
        dv_g = lax.dot_general(p_b, do, nn, preferred_element_type=f32)
        if g == 0:
            dk_ref[0], dv_ref[0] = dk_g, dv_g
        else:
            dk_ref[0] += dk_g
            dv_ref[0] += dv_g


def attention(q_proj, do, kv, prefix_len, base, cos_tab, sin_tab, scale):
    batch, tokens, width = q_proj.shape
    e = kv.shape[2] // 2
    n_keys = kv.shape[1]
    heads = width // e
    cos_one = jnp.concatenate([cos_tab, cos_tab], axis=1)
    sin_one = jnp.concatenate([-sin_tab, sin_tab], axis=1)
    cos_full = jnp.tile(cos_one, (GROUP_HEADS, 1))
    sin_full = jnp.tile(sin_one, (GROUP_HEADS, 1))
    rows = GROUP_HEADS * tokens
    tok_spec = pl.BlockSpec((1, tokens, width), lambda b, *_: (b, 0, 0))
    kv_spec = pl.BlockSpec((1, n_keys, 2 * e), lambda b, *_: (b, 0, 0))
    dk_spec = pl.BlockSpec((1, n_keys, e), lambda b, *_: (b, 0, 0))
    tab_spec = pl.BlockSpec((rows, e), lambda b, *_: (0, 0))
    tab_t_spec = pl.BlockSpec((e, rows), lambda b, *_: (0, 0))
    flops = 6 * 2 * batch * heads * tokens * n_keys * e
    return pl.pallas_call(
        functools.partial(attention_kernel, heads, scale),
        grid_spec=pltpu.PrefetchScalarGridSpec(
            num_scalar_prefetch=2,
            grid=(batch,),
            in_specs=[tok_spec, tok_spec, kv_spec, tab_spec, tab_spec, tab_t_spec, tab_t_spec],
            out_specs=[tok_spec, tok_spec, dk_spec, dk_spec],
            scratch_shapes=[pltpu.VMEM((n_keys, rows), jnp.float32)],
        ),
        out_shape=[
            jax.ShapeDtypeStruct((batch, tokens, width), jnp.bfloat16),
            jax.ShapeDtypeStruct((batch, tokens, width), jnp.bfloat16),
            jax.ShapeDtypeStruct((batch, n_keys, e), jnp.float32),
            jax.ShapeDtypeStruct((batch, n_keys, e), jnp.float32),
        ],
        cost_estimate=pl.CostEstimate(flops=2 * flops, bytes_accessed=q_proj.size * 10 + kv.size * 10, transcendentals=batch * heads * tokens * n_keys),
        compiler_params=pltpu.CompilerParams(dimension_semantics=("arbitrary",), vmem_limit_bytes=40 * 1024 * 1024),
        name="attention",
    )(prefix_len, base, q_proj, do, kv, cos_full, sin_full, cos_full.T, sin_full.T)


def solution(mesh):
    groups = mesh.shape['sp']
    seq_spec = P(None, 'sp', None)
    whole = P()

    def local_block(x, dy, prefix_len, w_norm, w_q, w_k, w_v, w_o):
        batch, tokens, d_model = x.shape
        head_dim = w_k.shape[1]
        scale = head_dim ** -0.5
        my_index = lax.axis_index('sp')
        f32 = jnp.float32

        x_f32 = x.astype(f32)
        normed_f32, norm_pull = jax.vjp(rms_norm, x_f32, w_norm.astype(f32))
        normed = normed_f32.astype(jnp.bfloat16)
        base = my_index * tokens
        cos_tab, sin_tab = rope_tables(base + jnp.arange(tokens), head_dim)
        k_own = apply_rope(jnp.einsum('bsd,de->bse', normed, w_k, preferred_element_type=f32), cos_tab, sin_tab).astype(jnp.bfloat16)
        v_own = jnp.einsum('bsd,de->bse', normed, w_v, preferred_element_type=f32).astype(jnp.bfloat16)
        kv = lax.all_gather(jnp.concatenate([k_own, v_own], axis=-1), 'sp', axis=1, tiled=True)
        q_proj = jnp.einsum('bsd,de->bse', normed, w_q, preferred_element_type=f32)
        do = jnp.einsum('bsd,ed->bse', dy, w_o, preferred_element_type=f32).astype(jnp.bfloat16)
        o, dq_proj, dk_part, dv_part = attention(q_proj, do, kv, prefix_len, base.reshape(1), cos_tab, sin_tab, scale)

        dkv_own = lax.psum_scatter(jnp.stack([dk_part, dv_part]), 'sp', scatter_dimension=2, tiled=True)
        dk_own = dkv_own[0].astype(jnp.bfloat16)
        dv_own = dkv_own[1].astype(jnp.bfloat16)
        d_wo = jnp.einsum('bse,bsd->ed', o, dy, preferred_element_type=f32)
        d_wq = jnp.einsum('bsd,bse->de', normed, dq_proj, preferred_element_type=f32)
        mixed = jnp.einsum('bse,ed->bsd', o, w_o, preferred_element_type=f32)
        y_out = (x_f32 + mixed).astype(jnp.bfloat16)

        dk_proj = apply_rope(dk_own.astype(f32), cos_tab, -sin_tab).astype(jnp.bfloat16)
        d_wk = jnp.einsum('bsd,bse->de', normed, dk_proj, preferred_element_type=f32)
        d_wv = jnp.einsum('bsd,bse->de', normed, dv_own, preferred_element_type=f32)
        d_normed = (jnp.einsum('bse,de->bsd', dq_proj, w_q, preferred_element_type=f32)
                    + jnp.einsum('bse,de->bsd', dk_proj, w_k, preferred_element_type=f32)
                    + jnp.einsum('bse,de->bsd', dv_own, w_v, preferred_element_type=f32))
        dx_norm, d_gain = norm_pull(d_normed.astype(jnp.bfloat16).astype(f32))
        dx_out = (dy.astype(f32) + dx_norm).astype(jnp.bfloat16)
        d_wo = lax.psum(d_wo, 'sp')
        d_wq = lax.psum(d_wq, 'sp')
        d_wk, d_wv, d_gain = lax.psum((d_wk, d_wv, d_gain), 'sp')
        return y_out, dx_out, d_wq, d_wk, d_wv, d_wo, d_gain

    return jax.shard_map(local_block, mesh=mesh, in_specs=(seq_spec, seq_spec, whole, whole, whole, whole, whole, whole), out_specs=(seq_spec, seq_spec, whole, whole, whole, whole, whole), check_vma=False)
```

time: 2560 us -> 1730 us (0.68)
  matrix products: 730 us -> 316 us
  other arithmetic: 301 us -> 34.7 us
  local copies, waits for them, and re-layouts: 285 us -> 97 us
  Pallas kernels: 0 us -> 94.4 us
  starting transfers between devices: 26.7 us -> 0.38 us
    dot_general x124 -> x12, matrix products: 730 us -> 316 us  [the longest x1 48.2 us: local_block(): jnp.einsum('bsd,bse->de', normed, dq_proj, preferred_element_type=f32)]
    sub x33 -> x0, other arithmetic: 212 us -> none  [the longest x16 97.3 us: attend_forward(): jax.nn.softmax(jnp.where(visible, scores, MASK_FILL), axis=-1)]
    all_to_all x4 -> x0, waiting for transfers between devices: 208 us -> none  [the longest x1 110 us: local_block(): o_seq = lax.all_to_all(o_heads, 'sp', 0, 0, tiled=True)]
    psum x2, waiting for transfers between devices: 918 us -> 1090 us  [the longest x1 627 us: local_block(): d_wq = lax.psum(d_wq, 'sp')]
    reshape x2 -> x0, local copies, waits for them, and re-layouts: 119 us -> none  [the longest x1 65.8 us: local_block(): jnp.einsum('bsd,gbshe->dghe', normed, dq_proj, preferred_element_type=jnp...]
    pallas_call x0 -> x1, Pallas kernels: none -> 94.4 us  [attention(): pl.pallas_call(functools.partial(attention_kernel, heads, scale), grid_sp...]
    reduce_scatter x2 -> x1, waiting for transfers between devices: 0.01 us -> 41.7 us  [local_block(): lax.psum_scatter(jnp.stack([dk_part, dv_part]), 'sp', scatter_dimension=2...]
    while x288 -> x0, local copies, waits for them, and re-layouts: 31.4 us -> none
  transfers between devices with their start and end apart: 10 -> 4, of which waited for: 4 -> 3; matrix products, arithmetic and copies ran while one was open for 29% -> 19% of each run, Pallas kernels for 0% -> 0%
where the time goes in v1:
time: 1730 us; the launch traced here: 1720 us
  waiting for transfers between devices  1130 us (65%)
  matrix products  316 us (18%)
  local copies, waits for them, and re-layouts  97 us (6%)
  Pallas kernels  94.4 us (5%)
  other arithmetic  34.7 us (2%)
  blocking collectives  31.7 us (2%)
    psum x1, waiting for transfers between devices, local_block(): d_wq = lax.psum(d_wq, 'sp')  627 us
    psum x1, waiting for transfers between devices, local_block(): d_wo = lax.psum(d_wo, 'sp')  462 us
    unnamed x60, local copies, waits for them, and re-layouts  96.8 us
    pallas_call x1, Pallas kernels, attention(): pl.pallas_call(functools.partial(attention_kernel, heads, scale), grid_sp...  94.4 us
    dot_general x1, matrix products, local_block(): jnp.einsum('bsd,bse->de', normed, dq_proj, preferred_element_type=f32)  48.2 us
    dot_general x1, matrix products, local_block(): d_wo = jnp.einsum('bse,bsd->ed', o, dy, preferred_element_type=f32)  47 us
    dot_general x1, matrix products, local_block(): jnp.einsum('bse,de->bsd', dq_proj, w_q, preferred_element_type=f32)  43.3 us
    dot_general x1, matrix products, local_block(): q_proj = jnp.einsum('bsd,de->bse', normed, w_q, preferred_element_type=f32)  43.3 us
  transfers between devices with their start and end apart: 4, of which 3 were waited for; matrix products, arithmetic and copies ran while one was open for 19% of the time, Pallas kernels for 0%

profile of v1, /device:TPU:0, one launch (start us, length us, event | category | flops | bytes accessed | tf_op | source)
XLA Modules:
  0.0 1719.6 jit_solution(12722291691914265850)
XLA Ops:
  7.2 0.0 copy-start
  7.2 0.0 copy-start.10
  7.2 0.0 all-gather.2.cloned.1.call-start
  7.3 0.0 slice-start
  7.3 0.9 convert_add_fusion.1
  8.1 5.5 fusion.14
  13.7 0.0 copy-start.17
  13.7 0.0 slice-start.1
  13.7 5.9 convolution_convert_fusion
  19.7 2.5 fusion.26
  22.2 0.1 fusion.30
  22.3 0.0 copy-start.20
  22.3 0.3 subtract_convert_fusion.1
  22.6 1.0 pad_maximum_fusion.1
  23.6 0.0 all-gather.2.cloned.1.call-update
  23.6 0.3 reduce-scatter.2.cloned.1.call-start
  23.9 0.1 pad_maximum_fusion.5
  24.0 0.1 copy.19
  24.1 0.1 copy.20
  24.2 43.3 %fusion.6.q_ref = f32[32,32,4096]{2,1,0:T(8,128)} fusion(bf16[4096,4096]{1,0:T(8,128)(2,1)} %param.12, bf16[32,32,4096]{2,1,0:T(8,128)(2,1)} %param.8, f32[4096]{0:T(1024)S(1)} %convert_add_fusion.1, f32[32,32]{1,0:T(8,128)S(1)} %fusion.29), kind=kOutput, calls=%fused_computation.8 | convolution fusion | flops 34376515584 | bytes 58740736 | tf_op jit(solution)/shard_map/bsd,de->bse/dot_general | solution.py:142
  67.5 42.7 %fusion.19.do_ref = bf16[32,32,4096]{2,1,0:T(8,128)(2,1)} fusion(bf16[32,32,4096]{2,1,0:T(8,128)(2,1)} %param.9, bf16[4096,4096]{1,0:T(8,128)(2,1)} %param.15), kind=kOutput, calls=%fused_computation.29 | convolution fusion | flops 34363932672 | bytes 50331648 | tf_op jit(solution)/shard_map/bsd,ed->bse/dot_general | solution.py:143
  110.3 0.0 copy-done.1
  110.3 94.4 %attention.1 = (bf16[32,32,4096]{2,1,0:T(8,128)(2,1)S(1)}, bf16[32,32,4096]{2,1,0:T(8,128)(2,1)}, f32[32,512,128]{2,1,0:T(8,128)}, f32[32,512,128]{2,1,0:T(8,128)}) custom-call(s32[32]{0:T(128)S(1)} %copy-done.1, s32[1]{0:T(128)} %bitcast.base_ref, f32[32,32,4096]{2,1,0:T(8,128)} %fusion.6.q_ref, bf16[32,32,4096]{2,1,0:T(8,128)(2,1)} %fusion.19.do_ref, ...), custom_call_target="tpu_custom_call" | custom-call | flops 51539607552 | bytes 83886080 | tf_op jit(solution)/shard_map/attention/pallas_call | solution.py:101
  204.7 3.4 copy-done.2
  208.1 11.5 pad_maximum_fusion
  219.6 0.0 reduce-scatter.2.cloned.1.call-update
  219.6 0.0 all-reduce.4.cloned.1.call-start
  219.7 47.0 %convolution_bitcast_fusion = f32[4096,4096]{1,0:T(8,128)} fusion(bf16[32,32,4096]{2,1,0:T(8,128)(2,1)} %copy-done.2, bf16[32,32,4096]{2,1,0:T(8,128)(2,1)} %param.9), kind=kOutput, calls=%fused_computation | convolution fusion | flops 34359738368 | bytes 83886080 | tf_op jit(solution)/shard_map/bse,bsd->ed/dot_general | solution.py:149
  266.6 0.0 all-reduce.4.cloned.1.call-update
  266.6 0.0 all-reduce.6.cloned.1.call-start
  266.7 0.0 copy-start.18
  266.7 43.3 %fusion.4 = f32[32,32,4096]{2,1,0:T(8,128)} fusion(bf16[32,32,4096]{2,1,0:T(8,128)(2,1)} %get-tuple-element.12, bf16[4096,4096]{1,0:T(8,128)(2,1)} %param.12), kind=kOutput, calls=%fused_computation.6 | convolution fusion | flops 34359738368 | bytes 58720256 | tf_op jit(solution)/shard_map/bse,de->bsd/dot_general | solution.py:157
  310.0 0.0 copy-start.21
  310.0 48.2 %convolution_bitcast_fusion.1 = f32[4096,4096]{1,0:T(8,128)} fusion(bf16[32,32,4096]{2,1,0:T(8,128)(2,1)} %get-tuple-element.12, bf16[32,32,4096]{2,1,0:T(8,128)(2,1)} %param.8, f32[4096]{0:T(1024)S(1)} %copy-done.15, f32[32,32]{1,0:T(8,128)S(1)} %copy-done.18), kind=kOutput, calls=%fused_computation.1 | convolution fusion | flops 34376515584 | bytes 83906560 | tf_op jit(solution)/shard_map/bsd,bse->de/dot_general | solution.py:150
  358.2 41.7 %reduce-scatter.2.cloned.1.call-done = f32[2,32,32,128]{3,2,1,0:T(8,128)} async-done(((f32[2,32,512,128]{3,2,1,0:T(8,128)}), f32[2,32,32,128]{3,2,1,0:T(8,128)}) %reduce-scatter.2.cloned.1.call-update) | async-done | bytes 1048592 | tf_op jit(solution)/shard_map/reduce_scatter | solution.py:146
  399.9 1.3 convert.19
  401.2 0.0 copy-start.3
  401.2 0.1 fusion.28
  401.3 0.0 slice-start.2
  401.3 0.2 subtract_convert_fusion
  401.6 0.7 copy-done.6
  402.3 8.3 convolution_bitcast_fusion.3
  410.6 0.0 copy-done.3
  410.6 4.6 convolution_bitcast_fusion.2
  415.3 0.0 all-reduce.6.cloned.1.call-update
  415.3 0.0 copy-start.11
  415.3 42.1 %fusion.15 = bf16[32,32,4096]{2,1,0:T(8,128)(2,1)} fusion(bf16[32,32,4096]{2,1,0:T(8,128)(2,1)} %param.8, bf16[32,32,4096]{2,1,0:T(8,128)(2,1)} %copy-done.2, bf16[4096,4096]{1,0:T(8,128)(2,1)} %param.15), kind=kOutput, calls=%fused_computation.25 | convolution fusion | flops 34372321280 | bytes 58720256 | tf_op jit(solution)/shard_map/bse,ed->bsd/dot_general | solution.py:151
  457.4 0.0 copy-done.9
  457.4 0.0 copy-done.11
  457.4 0.0 copy-start.4
  457.5 0.0 copy-start.16
  457.5 0.0 copy-start.19
  457.5 8.1 fusion.24
  465.6 0.0 copy-done.19
  465.6 19.7 %fusion.11 = (f32[4096]{0:T(1024)S(1)}, f32[32,32]{1,0:T(8,128)S(1)}, bf16[32,32,4096]{2,1,0:T(8,128)(2,1)}) fusion(bf16[32,32,4096]{2,1,0:T(8,128)(2,1)} %param.8, f32[32,32]{1,0:T(8,128)S(1)} %copy-done.19, f32[4096]{0:T(1024)S(1)} %copy-done.16, bf16[4096,128]{1,0:T(8,128)(2,1)S(1)} %copy-done, bf16[2,32,32,128]{3,2,1,0:T(8,128)(2,1)S(1)} %copy-done.4, ...), kind=kOutput, calls=%fused_computation.21 | convolution fusion | flops 1119874048 | bytes 51695616 | tf_op jit(solution)/shard_map/bse,de->bsd/dot_general | solution.py:159
  485.3 31.7 %psum.39 = f32[4096]{0:T(1024)} all-reduce(f32[4096]{0:T(1024)S(1)} %get-tuple-element.15), channel_id=1, replica_groups=mesh['sp'=16] {'sp'}, use_global_device_ids=true, to_apply=%region_8.0 | all-reduce | flops 4096 | bytes 32768 | tf_op jit(solution)/shard_map/psum | solution.py:164
  517.0 0.0 copy-done.23
  517.0 13.7 fusion.13
  530.7 461.8 %all-reduce.4.cloned.1.call-done = f32[4096,4096]{1,0:T(8,128)} async-done(((f32[4096,4096]{1,0:T(8,128)}), f32[4096,4096]{1,0:T(8,128)}) %all-reduce.4.cloned.1.call-update) | async-done | bytes 67108880 | tf_op jit(solution)/shard_map/psum | solution.py:162
  992.5 627.5 %all-reduce.6.cloned.1.call-done = (f32[4096,4096]{1,0:T(8,128)}, f32[4096,128]{1,0:T(8,128)}, f32[4096,128]{1,0:T(8,128)}) async-done(((f32[4096,4096]{1,0:T(8,128)}, f32[4096,128]{1,0:T(8,128)}, f32[4096,128]{1,0:T(8,128)}), (f32[4096,4096]{1,0:T(8,128)}, f32[4096,128]{1,0:T(8,128)}, f32[4096,128]{1,0:T(8,128)})) %all-reduce.6.cloned.1.call-update) | async-done | bytes 71303184 | tf_op jit(solution)/shard_map/psum | solution.py:163
  1620.0 44.1 %copy.25 = f32[4096,4096]{1,0:T(8,128)} copy(f32[4096,4096]{1,0:T(8,128)} %get-tuple-element.32) | data formatting | bytes 134217728
  1664.1 3.0 copy.26
  1667.2 1.3 copy.27
  1668.5 44.1 %copy.28 = f32[4096,4096]{1,0:T(8,128)} copy(f32[4096,4096]{1,0:T(8,128)} %all-reduce.4.cloned.1.call-done) | data formatting | bytes 134217728
  (43 shorter events, 0.1 us)
Async XLA Ops:
  7.2 6.5 copy-start
  7.2 12.5 copy-start.10
  7.2 103.1 %all-gather.2.cloned.1.call-start = ((), (), s32[]{:S(2)}) async-start(), calls=%async_computation.1 | async-start | bytes 8912896 | tf_op jit(solution)/shard_map/all_gather | solution.py:141
  7.3 12.4 slice-start
  8.1 16.1 copy-start.14
  13.7 8.5 copy-start.22
  13.7 10.5 copy-start.17
  13.7 5.9 slice-start.1
  22.3 1.7 copy-start.12
  22.3 1.7 copy-start.20
  23.6 376.3 %reduce-scatter.2.cloned.1.call-start = ((), (), s32[]{:S(2)}) async-start(), calls=%async_computation.2 | async-start | bytes 17825792 | tf_op jit(solution)/shard_map/reduce_scatter | solution.py:146
  67.5 42.7 %copy-start.1 = (s32[32]{0:T(128)S(1)}, s32[32]{0:T(128)}, u32[]{:S(2)}) copy-start(s32[32]{0:T(128)} %prefix_ref.1) | copy-start | bytes 388
  204.7 3.4 copy-start.2
  219.6 772.9 %all-reduce.4.cloned.1.call-start = ((), (), s32[]{:S(2)}) async-start(), calls=%async_computation.3 | async-start | bytes 134217728 | tf_op jit(solution)/shard_map/psum | solution.py:162
  266.6 1353.4 %all-reduce.6.cloned.1.call-start = ((), (), s32[]{:S(2)}) async-start(), calls=%async_computation.4 | async-start | bytes 142606336 | tf_op jit(solution)/shard_map/psum | solution.py:163
  266.7 43.3 %copy-start.15 = (f32[4096]{0:T(1024)S(1)}, f32[4096]{0:T(1024)}, u32[]{:S(2)}) copy-start(f32[4096]{0:T(1024)} %copy-done.14) | copy-start | bytes 49156
  266.7 43.3 %copy-start.18 = (f32[32,32]{1,0:T(8,128)S(1)}, f32[32,32]{1,0:T(8,128)}, u32[]{:S(2)}) copy-start(f32[32,32]{1,0:T(8,128)} %copy-done.17) | copy-start | bytes 12292
  310.0 91.2 %copy-start.13 = (f32[32,64]{1,0:T(8,128)S(1)}, f32[32,64]{1,0:T(8,128)}, u32[]{:S(2)}) copy-start(f32[32,64]{1,0:T(8,128)} %copy-done.12) | copy-start | bytes 24580
  310.0 91.3 %copy-start.21 = (f32[32,64]{1,0:T(8,128)S(1)}, f32[32,64]{1,0:T(8,128)}, u32[]{:S(2)}) copy-start(f32[32,64]{1,0:T(8,128)} %copy-done.20) | copy-start | bytes 24580
  401.2 9.4 copy-start.3
  401.3 9.3 slice-start.2
  401.6 0.7 copy-start.6
  401.6 9.0 copy-start.8
  402.3 8.3 slice-start.3
  415.3 42.1 %copy-start.7 = (bf16[32,32,64]{2,1,0:T(8,128)(2,1)S(1)}, bf16[32,32,64]{2,1,0:T(8,128)(2,1)}, u32[]{:S(2)}) copy-start(bf16[32,32,64]{2,1,0:T(8,128)(2,1)} %copy-done.6) | copy-start | bytes 393220
  415.3 42.1 %copy-start.9 = (bf16[32,32,64]{2,1,0:T(8,128)(2,1)S(1)}, bf16[32,32,64]{2,1,0:T(8,128)(2,1)}, u32[]{:S(2)}) copy-start(bf16[32,32,64]{2,1,0:T(8,128)(2,1)} %copy-done.8) | copy-start | bytes 393220
  415.3 42.1 %copy-start.11 = (bf16[4096,128]{1,0:T(8,128)(2,1)S(1)}, bf16[4096,128]{1,0:T(8,128)(2,1)}, u32[]{:S(2)}) copy-start(bf16[4096,128]{1,0:T(8,128)(2,1)} %param.13) | copy-start | bytes 3145732
  457.4 8.2 copy-start.4
  457.5 8.2 copy-start.16
  457.5 8.1 copy-start.19
  465.6 51.4 %copy-start.23 = (f32[32,32]{1,0:T(8,128)S(1)}, f32[32,32]{1,0:T(8,128)}, u32[]{:S(2)}) copy-start(f32[32,32]{1,0:T(8,128)} %copy-done.22) | copy-start | bytes 12292
  1620.0 47.2 %copy-start.5 = (f32[4096,128]{1,0:T(8,128)S(1)}, f32[4096,128]{1,0:T(8,128)}, u32[]{:S(2)}) copy-start(f32[4096,128]{1,0:T(8,128)} %get-tuple-element.34) | copy-start | bytes 6291460
Sparse Core Ops, SparseCore 0:
  23.8 54.2 all-gather.1
  219.7 180.1 reduce-scatter.1
  406.2 586.2 all-reduce.3
  999.4 620.5 all-reduce.5
